TPU v7x, 32 devices: a whole 2x2x4 slice. The times are simulated.
32 devices in a mesh: groups: 2 (over y), az: 4 (over z), rg: 2 (over x), acq: 2 (over core).
Axes of the slice: x: 2, y: 2, z: 4, core: 2. Of those that a mesh axis runs over, the one named last changes fastest.
Arguments:
- image_stack: bfloat16 [2, 64, 32, 4, 256], P(None, ('az', 'acq'), 'groups', 'rg'), parts along dimension 2, may hold values from -12 to 12
- steering: bfloat16 [4, 2, 64, 512], P('rg'), as said below
- wiener_filter: bfloat16 [4, 2, 64, 64], P('rg'), may hold values from -0.5 to 0.5
- range_group: int32 [4], P('rg'), may hold values from 0 to 3, as said below
- lay_list: int32 [32, 4, 32], P(('groups', 'az', 'acq'), 'rg'), parts along dimension 0, may hold values from 0 to 255, as said below
- lay_count: int32 [32, 4], P(('groups', 'az', 'acq'), 'rg'), parts along dimension 0, may hold values from 0 to 32, as said below
Outputs:
- power: bfloat16 [32, 4, 512, 256], P(('groups', 'az', 'acq'), 'rg'), parts along dimension 0
There are 2 independent parts, one for each index of `groups`. A program takes and returns all parts, laid end to end along the dimension named above; an argument that names none is the same for every part. Nothing has to cross between parts.
Inputs may be any that keep to these rules, and one draw needn't show every extreme that they name: `lay_list`: within one block the 32 entries are distinct pixels. The first lay_count entries of a block's list are its layover pixels; some block has 32. `range_group`: range block r belongs to a group from (r // 2) * 2 to (r // 2) * 2 + 1. `steering`: every complex entry has modulus 1 / sqrt(512) up to rounding.
All inputs are finite; a program needn't handle non-finite values.
Results may differ from a plain program's by a relative error of at most 0.0075.
Values may be sent and summed in bfloat16 or wider, within the bound.
No kernel may reach another device: no remote copies, remote signals or barrier semaphores. Data moves between devices by JAX's collectives and lax.ppermute only.
A program may use at most 64 MiB of HBM per device.

v0:
```python
import jax
import jax.numpy as jnp
from jax import lax
from jax.sharding import PartitionSpec as P

K = 64
E = 512
LMAX = 32
GRP_DEV = 2
ITERS = 8
STEP_SIZE = 0.5
SHRINK = 0.25
block_rows = 32


def complex_block(complex_parts):
    real_part = complex_parts[0]
    imag_part = complex_parts[1]
    upper = jnp.concatenate([real_part, -imag_part], axis=1)
    lower = jnp.concatenate([imag_part, real_part], axis=1)
    return jnp.concatenate([upper, lower], axis=0)


def ista_power(lane_data, operator):
    target = lane_data.astype(jnp.float32)
    elevation = operator.shape[1] // 2

    def sweep(sweep_index, estimate):
        rounded = estimate.astype(jnp.bfloat16)
        predicted = jnp.dot(rounded, operator.T, preferred_element_type=jnp.float32)
        misfit = (target - predicted).astype(jnp.bfloat16)
        update = estimate + STEP_SIZE * jnp.dot(
            misfit, operator, preferred_element_type=jnp.float32
        )
        magnitude = update[:, :elevation] ** 2 + update[:, elevation:] ** 2
        factor = jnp.maximum(1.0 - SHRINK * lax.rsqrt(jnp.maximum(magnitude, SHRINK * SHRINK)), 0.0)
        return update * jnp.concatenate([factor, factor], axis=1)

    start = jnp.zeros((lane_data.shape[0], 2 * elevation), jnp.float32)
    estimate = lax.fori_loop(0, ITERS, sweep, start)
    return (estimate[:, :elevation] ** 2 + estimate[:, elevation:] ** 2).astype(jnp.bfloat16)


def pack_order(usable):
    live_flags = usable.astype(jnp.int32)
    live_total = jnp.sum(live_flags)
    before_live = jnp.cumsum(live_flags) - live_flags
    before_empty = jnp.cumsum(1 - live_flags) - (1 - live_flags)
    lane_slot = jnp.where(usable, before_live, live_total + before_empty)
    source = (
        jnp.zeros_like(lane_slot).at[lane_slot].set(jnp.arange(lane_slot.shape[0], dtype=jnp.int32))
    )
    return (lane_slot, source, live_total)


def solve_lanes(lane_data, usable, operator):
    lane_slot, source, live_total = pack_order(usable)
    packed = jnp.take(lane_data, source, axis=0)
    lane_total = lane_data.shape[0]
    elevation = operator.shape[1] // 2

    def one_block(block_turn, result):
        row_block = lax.dynamic_slice_in_dim(packed, block_turn * block_rows, block_rows, 0)
        return lax.dynamic_update_slice_in_dim(
            result, ista_power(row_block, operator), block_turn * block_rows, 0
        )

    turns = (live_total + block_rows - 1) // block_rows
    result = lax.fori_loop(0, turns, one_block, jnp.zeros((lane_total, elevation), jnp.bfloat16))
    return jnp.take(result, lane_slot, axis=0)


def shards(image_stack, steering, wiener_filter, range_group, lay_list, lay_count):
    halves, acq_share, azb_all, range_local, block_pixels = image_stack.shape
    relaid = lax.all_to_all(
        image_stack.reshape(halves, 1, acq_share, azb_all, range_local, block_pixels),
        ("az", "acq"),
        split_axis=3,
        concat_axis=1,
        tiled=True,
    )
    blocks = lay_list.shape[0]
    pixels = relaid.reshape(2 * K, blocks, range_local, block_pixels)
    first_group = lax.axis_index("rg") * GRP_DEV
    operators = []
    wiener_sets = []
    lane_sets = []
    usable_sets = []
    chosen_sets = []
    for column in range(range_local):
        pick_group = jnp.arange(GRP_DEV, dtype=jnp.int32) == range_group[column] - first_group
        steer_parts = jnp.sum(
            jnp.where(pick_group[:, None, None, None], steering, jnp.zeros_like(steering)), axis=0
        )
        filter_parts = jnp.sum(
            jnp.where(
                pick_group[:, None, None, None], wiener_filter, jnp.zeros_like(wiener_filter)
            ),
            axis=0,
        )
        operator = complex_block(steer_parts)
        filter_matrix = complex_block(filter_parts)
        block_data = pixels[:, :, column, :]
        filtered = jnp.einsum(
            "ij,jap->iap", filter_matrix, block_data, preferred_element_type=jnp.float32
        ).astype(jnp.bfloat16)
        beamed = jnp.einsum("ie,iap->aep", operator, filtered, preferred_element_type=jnp.float32)
        wiener_sets.append(beamed[:, :E] ** 2 + beamed[:, E:] ** 2)
        listed = lay_list[:, column, :]
        live_count = lay_count[:, column]
        usable = jnp.arange(LMAX, dtype=jnp.int32)[None, :] < live_count[:, None]
        chosen = (
            (listed[:, :, None] == jnp.arange(block_pixels, dtype=jnp.int32)[None, None, :])
            & usable[:, :, None]
        ).astype(jnp.bfloat16)
        lane_data = jnp.einsum(
            "alp,iap->ali", chosen, block_data, preferred_element_type=jnp.float32
        ).astype(jnp.bfloat16)
        operators.append(operator)
        lane_sets.append(lane_data.reshape(blocks * LMAX, 2 * K))
        usable_sets.append(usable.reshape(blocks * LMAX))
        chosen_sets.append(chosen)
    powers = [
        solve_lanes(lane_sets[column], usable_sets[column], operators[column])
        for column in range(range_local)
    ]
    outputs = []
    for column in range(range_local):
        lay_power = powers[column].reshape(blocks, LMAX, E)
        placed = jnp.einsum(
            "alp,ale->aep", chosen_sets[column], lay_power, preferred_element_type=jnp.float32
        )
        covered = jnp.sum(chosen_sets[column].astype(jnp.float32), axis=1)
        outputs.append(
            jnp.where(covered[:, None, :] > 0.5, placed, wiener_sets[column]).astype(jnp.bfloat16)
        )
    return jnp.stack(outputs, axis=1)


def solution(mesh):
    return jax.shard_map(
        shards,
        mesh=mesh,
        in_specs=(
            P(None, ("az", "acq"), "groups", "rg", None),
            P("rg", None, None, None),
            P("rg", None, None, None),
            P("rg"),
            P(("groups", "az", "acq"), "rg", None),
            P(("groups", "az", "acq"), "rg"),
        ),
        out_specs=P(("groups", "az", "acq"), "rg", None, None),
        check_vma=False,
    )
```

profile of v0, /device:TPU:27, one launch (start us, length us, event | category | flops | bytes accessed | tf_op | source)
XLA Modules:
  0.0 42.8 jit_solution(8267527143187497523)
XLA Ops:
  0.0 1.9 %copy.39 = bf16[2,8,16,2,256]{4,3,1,0,2:T(2,128)(2,1)} copy(bf16[2,8,16,2,256]{4,3,2,1,0:T(2,128)(2,1)} %param.18) | data formatting | bytes 524288 | tf_op args[0]
  1.9 5.4 %all-to-all-start = ((bf16[2,1,8,16,2,256]{5,4,2,0,1,3:T(2,128)(2,1)}), bf16[2,1,8,16,2,256]{5,4,2,0,1,3:T(2,128)(2,1)S(1)}, u32[]{:S(2)}, u32[]{:S(2)}) async-start(bf16[2,1,8,16,2,256]{5,4,2,0,1,3:T(2,128)(2,1)} %bitcast.76), calls=%async_computation | async-start | bytes 524288 | tf_op jit(solution)/shard_map/all_to_all | solution.py:75
  7.3 1.0 %slice_reduce_fusion.1 = (s32[2]{0:T(128)S(1)}, s32[2]{0:T(128)S(1)}) fusion(s32[2,2]{1,0:T(2,128)} %param.23), kind=kLoop, calls=%fused_computation.142 | loop fusion | bytes 32 | tf_op jit(solution)/shard_map/slice | solution.py:110
  8.3 0.7 %convert_reduce_fusion.3 = s32[]{:T(128)} fusion(s32[2]{0:T(128)S(1)} %get-tuple-element.175), kind=kLoop, calls=%fused_computation.139 | loop fusion | flops 191 | bytes 12 | tf_op jit(solution)/shard_map/reduce_sum | solution.py:46
  9.1 0.1 lt.160
  9.3 0.1 lt.161
  9.4 0.8 %convert_reduce_fusion.2 = s32[]{:T(128)} fusion(s32[2]{0:T(128)S(1)} %get-tuple-element.176), kind=kLoop, calls=%fused_computation.136 | loop fusion | flops 191 | bytes 12 | tf_op jit(solution)/shard_map/reduce_sum | solution.py:46
  10.6 1.4 %fusion.92 = (s32[64]{0:T(128)S(1)}, s32[64]{0:T(128)S(1)}, s32[64]{0:T(128)S(1)}, s32[64]{0:T(128)S(1)}, s32[64]{0:T(128)S(1)}, /*index=5*/s32[64]{0:T(128)S(1)}) fusion(s32[64,1]{1,0:T(8,128)S(1)} %reduce-window.14, pred[64,1]{1,0:T(8,128)(4,1)S(1)} %lt.160, s32[64,1]{1,0:T(8,128)S(1)} %reduce-window.15, s32[]{:T(128)} %convert_reduce_fusion.3, ...), kind=kLoop, calls=%fused_computation.156 | loop fusion | flops 1152 | bytes 2696 | tf_op jit(solution)/shard_map/reduce-window
  12.0 0.8 %scatter_custom_fusion = s32[64]{0:T(128)S(1)} fusion(s32[64]{0:T(128)S(1)} %get-tuple-element.170, s32[64]{0:T(128)S(1)} %iota.35, s32[]{:T(128)} %constant.130.clone.1), kind=kCustom, calls=%fused_computation.148 | custom fusion | bytes 260 | tf_op jit(solution)/shard_map/scatter | solution.py:51
  12.8 1.3 %fusion.95 = (s32[1]{0:T(128)}, s32[1]{0:T(128)}) fusion(s32[2]{0:T(128)} %param.21), kind=kLoop, calls=%fused_computation.159 | loop fusion | bytes 16 | tf_op jit(solution)/shard_map/slice | solution.py:91
  15.5 1.1 %select_reduce_fusion.1 = (bf16[2,64,512]{2,1,0:T(8,128)(2,1)S(1)}, bf16[2,64,512]{2,1,0:T(8,128)(2,1)S(1)}) fusion(bf16[2,2,64,512]{3,2,1,0:T(8,128)(2,1)} %param.19, pred[2]{0:T(512)(128)(4,1)S(1)} %iota_compare_fusion.5, pred[2]{0:T(512)(128)(4,1)S(1)} %iota_compare_fusion.4), kind=kLoop, calls=%fused_computation.71 | loop fusion | flops 393216 | bytes 524292 | tf_op jit(solution)/shard_map/reduce_sum | solution.py:92
  16.7 0.8 %scatter_custom_fusion.1 = s32[64]{0:T(128)S(1)} fusion(s32[64]{0:T(128)S(1)} %get-tuple-element.230, s32[64]{0:T(128)S(1)} %iota.37, s32[]{:T(128)} %constant.130.clone.1), kind=kCustom, calls=%fused_computation.146 | custom fusion | bytes 260 | tf_op jit(solution)/shard_map/scatter | solution.py:51
  17.7 0.6 %compare_and_fusion.2 = (pred[64]{0:T(512)(128)(4,1)S(1)}, s32[64]{0:T(128)S(1)}) fusion(pred[64]{0:T(512)(128)(4,1)S(1)} %lt.139, s32[64]{0:T(128)S(1)} %get-tuple-element.171, s32[]{:T(128)} %convert_reduce_fusion.3, s32[64]{0:T(128)S(1)} %get-tuple-element.169), kind=kLoop, calls=%fused_computation.134 | loop fusion | flops 768 | bytes 900 | tf_op jit(solution)/shard_map/jit(_take)/and | solution.py:70
  18.6 0.7 %compare_and_fusion = (pred[64]{0:T(512)(128)(4,1)S(1)}, s32[64]{0:T(128)S(1)}) fusion(pred[64]{0:T(512)(128)(4,1)S(1)} %lt.145, s32[64]{0:T(128)S(1)} %get-tuple-element.229, s32[]{:T(128)} %convert_reduce_fusion.2, s32[64]{0:T(128)S(1)} %get-tuple-element.231), kind=kLoop, calls=%fused_computation.132 | loop fusion | flops 768 | bytes 900 | tf_op jit(solution)/shard_map/jit(_take)/and | solution.py:70
  20.7 0.2 convolution_convert_fusion.3
  20.9 0.2 convolution_convert_fusion.2
  21.1 0.6 %gather_fusion = bf16[64,128]{1,0:T(8,128)(2,1)S(1)} fusion(bf16[64,128]{1,0:T(8,128)(2,1)S(1)} %bitcast.90, s32[1024]{0:T(1024)S(1)} %pad_clamp_fusion.3), kind=kCustom, calls=%fused_computation.clone | custom fusion | bytes 33024 | tf_op jit(solution)/shard_map/jit(_take)/gather | solution.py:58
  21.9 7.7 %while.47 = (s32[]{:T(128)}, bf16[64,512]{1,0:T(8,128)(2,1)S(1)}, s32[]{:T(128)}, bf16[64,128]{1,0:T(8,128)(2,1)S(1)}, bf16[128,1024]{1,0:T(8,128)(2,1)S(1)}, /*...) while((s32[]{:T(128)}, bf16[64,512]{1,0:T(8,128)(2,1)S(1)}, ...), condition=%wide.region_9.11_spmd, body=%wide.region_6.10_spmd.sunk | while | flops 17199112 | bytes 1253674 | solution.py:69
  21.9 3.8 %while.50 = (s32[]{:T(128)}, f32[32,1024]{1,0:T(8,128)S(1)}, bf16[128,1024]{1,0:T(8,128)(2,1)S(1)}, f32[32,128]{1,0:T(8,128)S(1)}, s32[]{:T(128)}, /*index=5*/s32[]{:T(128)}) while((s32[]{:T(128)}, f32[32,1024]{1,0:T(8,128)S(1)}, bf16[128,1024]{1,0:T(8,128)(2,1)S(1)}, f32[32,128]{1,0:T(8,128)S(1)}, s32[]{:T(128)}, ...), condition=%wide.region_8.9_spmd.clone, body=%wide.region_7.8_spmd.clone.sunk | while | flops 17129476 | bytes 1065039 | solution.py:40
  21.9 0.4 fusion.120
  22.4 0.4 fusion.120
  22.9 0.4 fusion.120
  23.4 0.4 fusion.120
  23.8 0.4 fusion.120
  24.3 0.4 fusion.120
  24.8 0.4 fusion.120
  25.2 0.4 fusion.120
  25.8 3.8 %while.50 = (s32[]{:T(128)}, f32[32,1024]{1,0:T(8,128)S(1)}, bf16[128,1024]{1,0:T(8,128)(2,1)S(1)}, f32[32,128]{1,0:T(8,128)S(1)}, s32[]{:T(128)}, /*index=5*/s32[]{:T(128)}) while((s32[]{:T(128)}, f32[32,1024]{1,0:T(8,128)S(1)}, bf16[128,1024]{1,0:T(8,128)(2,1)S(1)}, f32[32,128]{1,0:T(8,128)S(1)}, s32[]{:T(128)}, ...), condition=%wide.region_8.9_spmd.clone, body=%wide.region_7.8_spmd.clone.sunk | while | flops 17129476 | bytes 1065039 | solution.py:40
  25.8 0.4 fusion.120
  26.3 0.4 fusion.120
  26.7 0.4 fusion.120
  27.2 0.4 fusion.120
  27.7 0.4 fusion.120
  28.2 0.4 fusion.120
  28.6 0.4 fusion.120
  29.1 0.4 fusion.120
  29.6 0.6 %gather_fusion.2 = bf16[64,128]{1,0:T(8,128)(2,1)S(1)} fusion(bf16[64,128]{1,0:T(8,128)(2,1)S(1)} %bitcast.89, s32[1024]{0:T(1024)S(1)} %pad_clamp_fusion.1), kind=kCustom, calls=%fused_computation.2.clone | custom fusion | bytes 33024 | tf_op jit(solution)/shard_map/jit(_take)/gather | solution.py:58
  30.3 7.7 %while.49 = (s32[]{:T(128)}, bf16[64,512]{1,0:T(8,128)(2,1)S(1)}, s32[]{:T(128)}, bf16[64,128]{1,0:T(8,128)(2,1)S(1)}, bf16[128,1024]{1,0:T(8,128)(2,1)S(1)}, /*...) while((s32[]{:T(128)}, bf16[64,512]{1,0:T(8,128)(2,1)S(1)}, ...), condition=%wide.region_20.23_spmd, body=%wide.region_17.22_spmd.sunk | while | flops 17199112 | bytes 1253674 | solution.py:69
  30.4 3.8 %while.51 = (s32[]{:T(128)}, f32[32,1024]{1,0:T(8,128)S(1)}, bf16[128,1024]{1,0:T(8,128)(2,1)S(1)}, f32[32,128]{1,0:T(8,128)S(1)}, s32[]{:T(128)}, /*index=5*/s32[]{:T(128)}) while((s32[]{:T(128)}, f32[32,1024]{1,0:T(8,128)S(1)}, bf16[128,1024]{1,0:T(8,128)(2,1)S(1)}, f32[32,128]{1,0:T(8,128)S(1)}, s32[]{:T(128)}, ...), condition=%wide.region_19.21_spmd.clone, body=%wide.region_18.20_spmd.clone.sunk | while | flops 17129476 | bytes 1065039 | solution.py:40
  30.4 0.4 fusion.116
  30.9 0.4 fusion.116
  31.3 0.4 fusion.116
  31.8 0.4 fusion.116
  32.3 0.4 fusion.116
  32.8 0.4 fusion.116
  33.2 0.4 fusion.116
  33.7 0.4 fusion.116
  34.2 3.8 %while.51 = (s32[]{:T(128)}, f32[32,1024]{1,0:T(8,128)S(1)}, bf16[128,1024]{1,0:T(8,128)(2,1)S(1)}, f32[32,128]{1,0:T(8,128)S(1)}, s32[]{:T(128)}, /*index=5*/s32[]{:T(128)}) while((s32[]{:T(128)}, f32[32,1024]{1,0:T(8,128)S(1)}, bf16[128,1024]{1,0:T(8,128)(2,1)S(1)}, f32[32,128]{1,0:T(8,128)S(1)}, s32[]{:T(128)}, ...), condition=%wide.region_19.21_spmd.clone, body=%wide.region_18.20_spmd.clone.sunk | while | flops 17129476 | bytes 1065039 | solution.py:40
  34.3 0.4 fusion.116
  34.7 0.4 fusion.116
  35.2 0.4 fusion.116
  35.7 0.4 fusion.116
  36.1 0.4 fusion.116
  36.6 0.4 fusion.116
  37.1 0.4 fusion.116
  37.6 0.4 fusion.116
  38.1 0.7 %gather_fusion.1 = bf16[64,512]{1,0:T(8,128)(2,1)S(1)} fusion(bf16[64,512]{1,0:T(8,128)(2,1)S(1)} %get-tuple-element.133, s32[1024]{0:T(1024)S(1)} %pad_clamp_fusion.2), kind=kCustom, calls=%fused_computation.1.clone | custom fusion | bytes 131328 | tf_op jit(solution)/shard_map/jit(_take)/gather | solution.py:70
  38.8 0.7 %gather_fusion.3 = bf16[64,512]{1,0:T(8,128)(2,1)S(1)} fusion(bf16[64,512]{1,0:T(8,128)(2,1)S(1)} %get-tuple-element.134, s32[1024]{0:T(1024)S(1)} %pad_clamp_fusion), kind=kCustom, calls=%fused_computation.3.clone | custom fusion | bytes 131328 | tf_op jit(solution)/shard_map/jit(_take)/gather | solution.py:70
  39.6 0.6 %convolution_bitcast_fusion.1 = f32[2,1024,256]{2,1,0:T(8,128)S(1)} fusion(bf16[128,2,2,256]{3,0,1,2:T(8,128)(2,1)S(1)} %bitcast.87, bf16[64,64]{1,0:T(8,128)(2,1)S(1)} %get-tuple-element.236, bf16[64,64]{1,0:T(8,128)(2,1)S(1)} %get-tuple-element.237, bf16[64,64]{1,0:T(8,128)(2,1)S(1)} %get-tuple-element.238, bf16[64,512]{1,0:T(8,128)(2,1)S(1)} %get-tuple-element.232, ...), kind=kOutput, calls=%fused_computation.47 | convolution fusion | flops 152240128 | bytes 2473984 | tf_op jit(solution)/shard_map/ie,iap->aep/dot_general | solution.py:107
  40.3 0.4 fusion.33
  40.7 0.6 %convolution_bitcast_fusion = f32[2,1024,256]{2,1,0:T(8,128)S(1)} fusion(bf16[128,2,2,256]{3,0,1,2:T(8,128)(2,1)S(1)} %bitcast.88, bf16[64,64]{1,0:T(8,128)(2,1)S(1)} %get-tuple-element.224, bf16[64,64]{1,0:T(8,128)(2,1)S(1)} %get-tuple-element.223, bf16[64,64]{1,0:T(8,128)(2,1)S(1)} %get-tuple-element.239, bf16[64,512]{1,0:T(8,128)(2,1)S(1)} %get-tuple-element.220, ...), kind=kOutput, calls=%fused_computation.46 | convolution fusion | flops 152240128 | bytes 2473984 | tf_op jit(solution)/shard_map/ie,iap->aep/dot_general | solution.py:107
  41.3 0.4 fusion.32
  41.7 0.1 pad_maximum_fusion
  41.8 1.0 %copy.33 = bf16[2,2,512,256]{3,2,1,0:T(8,128)(2,1)} copy(bf16[2,2,512,256]{3,2,0,1:T(8,128)(2,1)S(1)} %pad_maximum_fusion) | data formatting | bytes 2097152 | tf_op jit(solution)/shard_map/stack | solution.py:137
  (124 shorter events, 3.0 us)
Async XLA Ops:
  0.0 17.6 %copy-start.1 = (s32[2,2,32]{2,1,0:T(2,128)S(1)}, s32[2,2,32]{2,1,0:T(2,128)}, u32[]{:S(2)}) copy-start(s32[2,2,32]{2,1,0:T(2,128)} %param.22) | copy-start | bytes 1540
  0.0 18.3 %copy-start = (bf16[2,2,64,64]{3,2,1,0:T(8,128)(2,1)S(1)}, bf16[2,2,64,64]{3,2,1,0:T(8,128)(2,1)}, u32[]{:S(2)}) copy-start(bf16[2,2,64,64]{3,2,1,0:T(8,128)(2,1)} %param.20) | copy-start | bytes 98308
  1.9 18.8 %all-to-all-start = ((bf16[2,1,8,16,2,256]{5,4,2,0,1,3:T(2,128)(2,1)}), bf16[2,1,8,16,2,256]{5,4,2,0,1,3:T(2,128)(2,1)S(1)}, u32[]{:S(2)}, u32[]{:S(2)}) async-start(bf16[2,1,8,16,2,256]{5,4,2,0,1,3:T(2,128)(2,1)} %bitcast.76), calls=%async_computation | async-start | bytes 524288 | tf_op jit(solution)/shard_map/all_to_all | solution.py:75
where the time goes:
time: 43.2 us; the launch traced here: 42.8 us
  matrix products  15 us (35%)
  local copies, waits for them, and re-layouts  9.99 us (23%)
  other arithmetic  8.13 us (19%)
  starting transfers between devices  5.38 us (12%)
  between operations  2.9 us (7%)
  loops' own time  1.45 us (3%)
    dot_general x32, matrix products, sweep(): jnp.dot(misfit, operator, preferred_element_type=jnp.float32)  12.6 us
    all_to_all x1, starting transfers between devices, shards(): lax.all_to_all(image_stack.reshape(halves, 1, acq_share, azb_all, range_l...  5.38 us
    unnamed x5, local copies, waits for them, and re-layouts  1.93 us
    another operation x5, other arithmetic  1.82 us
    scatter x2, local copies, waits for them, and re-layouts, pack_order(): jnp.zeros_like(lane_slot).at[lane_slot]  1.55 us
    reduce_sum x2, other arithmetic, pack_order(): live_total = jnp.sum(live_flags)  1.48 us
    gather x2, local copies, waits for them, and re-layouts, solve_lanes(): return jnp.take(result, lane_slot, axis=0)  1.4 us
    slice x1, local copies, waits for them, and re-layouts, shards(): range_group[column] - first_group  1.34 us
  transfers between devices with their start and end apart: 1, of which 0 were waited for; matrix products, arithmetic and copies ran while one was open for 25% of the time, Pallas kernels for 0%

commit v1 on v0

--- a/solution.py
+++ b/solution.py
@@ -72,12 +72,20 @@
 
 def shards(image_stack, steering, wiener_filter, range_group, lay_list, lay_count):
     halves, acq_share, azb_all, range_local, block_pixels = image_stack.shape
-    relaid = lax.all_to_all(
-        image_stack.reshape(halves, 1, acq_share, azb_all, range_local, block_pixels),
-        ("az", "acq"),
-        split_axis=3,
-        concat_axis=1,
-        tiled=True,
+    relaid = jnp.concatenate(
+        lax.all_to_all(
+            jnp.stack(
+                jnp.split(
+                    image_stack.reshape(halves, 1, acq_share, azb_all, range_local, block_pixels),
+                    lax.axis_size(("az", "acq")),
+                    axis=3,
+                )
+            ),
+            ("az", "acq"),
+            0,
+            0,
+        ),
+        axis=1,
     )
     blocks = lay_list.shape[0]
     pixels = relaid.reshape(2 * K, blocks, range_local, block_pixels)

time: 43.2 us -> 53 us (1.23)
  local copies, waits for them, and re-layouts: 9.99 us -> 19.3 us
    unnamed x5 -> x11, local copies, waits for them, and re-layouts: 1.93 us -> 9.82 us
    another operation x2 -> x3, local copies, waits for them, and re-layouts: 0.01 us -> 1.41 us  [the longest x1 1.4 us: shards(): jnp.stack(jnp.split(image_stack.reshape(halves, 1, acq_share, azb_all, ra...]
  transfers between devices with their start and end apart: 1 -> 1, of which waited for: 0 -> 0; matrix products, arithmetic and copies ran while one was open for 25% -> 20% of each run, Pallas kernels for 0% -> 0%
where the time goes in v1:
time: 53 us; the launch traced here: 52.2 us
  local copies, waits for them, and re-layouts  19.3 us (36%)
  matrix products  15.1 us (28%)
  other arithmetic  8.12 us (15%)
  starting transfers between devices  5.38 us (10%)
  between operations  2.89 us (5%)
  loops' own time  1.45 us (3%)
    dot_general x32, matrix products, sweep(): jnp.dot(misfit, operator, preferred_element_type=jnp.float32)  12.6 us
    unnamed x11, local copies, waits for them, and re-layouts  9.82 us
    all_to_all x1, starting transfers between devices, shards(): lax.all_to_all(jnp.stack(jnp.split(image_stack.reshape(halves, 1, acq_sha...  5.38 us
    another operation x5, other arithmetic  1.82 us
    scatter x2, local copies, waits for them, and re-layouts, pack_order(): jnp.zeros_like(lane_slot).at[lane_slot]  1.55 us
    reduce_sum x2, other arithmetic, pack_order(): live_total = jnp.sum(live_flags)  1.47 us
    gather x2, local copies, waits for them, and re-layouts, solve_lanes(): return jnp.take(result, lane_slot, axis=0)  1.4 us
    another operation x1, local copies, waits for them, and re-layouts, shards(): jnp.stack(jnp.split(image_stack.reshape(halves, 1, acq_share, azb_all, ra...  1.4 us
  transfers between devices with their start and end apart: 1, of which 0 were waited for; matrix products, arithmetic and copies ran while one was open for 20% of the time, Pallas kernels for 0%

profile of v1, /device:TPU:27, one launch (start us, length us, event | category | flops | bytes accessed | tf_op | source)
XLA Modules:
  0.0 52.2 jit_solution(9373766455832461404)
XLA Ops:
  0.0 1.4 %fusion.55 = bf16[8,2,1,8,2,2,256]{6,5,4,3,1,2,0:T(2,128)(2,1)} fusion(bf16[2,1,8,16,2,256]{5,4,3,2,0,1:T(2,128)(2,1)} %bitcast.120), kind=kLoop, calls=%fused_computation.108 | loop fusion | bytes 65536
  1.4 1.4 %fusion.54 = bf16[8,2,1,8,2,2,256]{6,5,4,3,1,2,0:T(2,128)(2,1)} fusion(bf16[8,2,1,8,2,2,256]{6,5,4,3,1,2,0:T(2,128)(2,1)} %fusion.55, bf16[2,1,8,16,2,256]{5,4,3,2,0,1:T(2,128)(2,1)} %bitcast.121), kind=kLoop, calls=%fused_computation.106 | loop fusion | bytes 65536
  2.8 1.4 %fusion.53 = bf16[8,2,1,8,2,2,256]{6,5,4,3,1,2,0:T(2,128)(2,1)} fusion(bf16[8,2,1,8,2,2,256]{6,5,4,3,1,2,0:T(2,128)(2,1)} %fusion.54, bf16[2,1,8,16,2,256]{5,4,3,2,0,1:T(2,128)(2,1)} %bitcast.122), kind=kLoop, calls=%fused_computation.104 | loop fusion | bytes 65536
  4.2 1.4 %fusion.52 = bf16[8,2,1,8,2,2,256]{6,5,4,3,1,2,0:T(2,128)(2,1)} fusion(bf16[8,2,1,8,2,2,256]{6,5,4,3,1,2,0:T(2,128)(2,1)} %fusion.53, bf16[2,1,8,16,2,256]{5,4,3,2,0,1:T(2,128)(2,1)} %bitcast.123), kind=kLoop, calls=%fused_computation.102 | loop fusion | bytes 65536
  5.6 1.4 %fusion.51 = bf16[8,2,1,8,2,2,256]{6,5,4,3,1,2,0:T(2,128)(2,1)} fusion(bf16[8,2,1,8,2,2,256]{6,5,4,3,1,2,0:T(2,128)(2,1)} %fusion.52, bf16[2,1,8,16,2,256]{5,4,3,2,0,1:T(2,128)(2,1)} %bitcast.124), kind=kLoop, calls=%fused_computation.100 | loop fusion | bytes 65536
  7.0 1.4 %fusion.50 = bf16[8,2,1,8,2,2,256]{6,5,4,3,1,2,0:T(2,128)(2,1)} fusion(bf16[8,2,1,8,2,2,256]{6,5,4,3,1,2,0:T(2,128)(2,1)} %fusion.51, bf16[2,1,8,16,2,256]{5,4,3,2,0,1:T(2,128)(2,1)} %bitcast.125), kind=kLoop, calls=%fused_computation.98 | loop fusion | bytes 65536
  8.4 1.4 %fusion.49 = bf16[8,2,1,8,2,2,256]{6,5,4,3,1,2,0:T(2,128)(2,1)} fusion(bf16[8,2,1,8,2,2,256]{6,5,4,3,1,2,0:T(2,128)(2,1)} %fusion.50, bf16[2,1,8,16,2,256]{5,4,3,2,0,1:T(2,128)(2,1)} %bitcast.126), kind=kLoop, calls=%fused_computation.96 | loop fusion | bytes 65536
  9.8 1.4 %fusion.48 = bf16[8,2,1,8,2,2,256]{6,5,4,3,1,2,0:T(2,128)(2,1)} fusion(bf16[8,2,1,8,2,2,256]{6,5,4,3,1,2,0:T(2,128)(2,1)} %fusion.49, bf16[2,1,8,16,2,256]{5,4,3,2,0,1:T(2,128)(2,1)} %bitcast.127), kind=kLoop, calls=%fused_computation.94 | loop fusion | bytes 65536 | tf_op jit(solution)/shard_map/stack | solution.py:77
  11.2 5.4 %all-to-all-start = ((bf16[8,2,1,8,2,2,256]{6,5,4,3,1,2,0:T(2,128)(2,1)}), bf16[8,2,1,8,2,2,256]{6,5,4,3,1,2,0:T(2,128)(2,1)S(1)}, u32[]{:S(2)}, u32[]{:S(2)}) async-start(bf16[8,2,1,8,2,2,256]{6,5,4,3,1,2,0:T(2,128)(2,1)} %fusion.48), calls=%async_computation | async-start | bytes 524288 | tf_op jit(solution)/shard_map/all_to_all | solution.py:76
  16.6 1.0 %slice_reduce_fusion.1 = (s32[2]{0:T(128)S(1)}, s32[2]{0:T(128)S(1)}) fusion(s32[2,2]{1,0:T(2,128)} %param.23), kind=kLoop, calls=%fused_computation.157 | loop fusion | bytes 32 | tf_op jit(solution)/shard_map/slice | solution.py:118
  18.0 0.8 %convert_reduce_fusion.2 = s32[]{:T(128)} fusion(s32[2]{0:T(128)S(1)} %get-tuple-element.176), kind=kLoop, calls=%fused_computation.151 | loop fusion | flops 191 | bytes 12 | tf_op jit(solution)/shard_map/reduce_sum | solution.py:46
  18.8 0.7 %convert_reduce_fusion.3 = s32[]{:T(128)} fusion(s32[2]{0:T(128)S(1)} %get-tuple-element.175), kind=kLoop, calls=%fused_computation.154 | loop fusion | flops 191 | bytes 12 | tf_op jit(solution)/shard_map/reduce_sum | solution.py:46
  19.9 1.4 %fusion.100 = (s32[64]{0:T(128)S(1)}, s32[64]{0:T(128)S(1)}, s32[64]{0:T(128)S(1)}, s32[64]{0:T(128)S(1)}, s32[64]{0:T(128)S(1)}, /*index=5*/s32[64]{0:T(128)S(1)}) fusion(s32[64,1]{1,0:T(8,128)S(1)} %reduce-window.14, pred[64,1]{1,0:T(8,128)(4,1)S(1)} %lt.160, s32[64,1]{1,0:T(8,128)S(1)} %reduce-window.15, s32[]{:T(128)} %convert_reduce_fusion.3, ...), kind=kLoop, calls=%fused_computation.171 | loop fusion | flops 1152 | bytes 2696 | tf_op jit(solution)/shard_map/reduce-window
  21.3 0.8 %scatter_custom_fusion = s32[64]{0:T(128)S(1)} fusion(s32[64]{0:T(128)S(1)} %get-tuple-element.170, s32[64]{0:T(128)S(1)} %iota.35, s32[]{:T(128)} %constant.130.clone.1), kind=kCustom, calls=%fused_computation.163 | custom fusion | bytes 260 | tf_op jit(solution)/shard_map/scatter | solution.py:51
  22.1 1.3 %fusion.103 = (s32[1]{0:T(128)}, s32[1]{0:T(128)}) fusion(s32[2]{0:T(128)} %param.21), kind=kLoop, calls=%fused_computation.174 | loop fusion | bytes 16 | tf_op jit(solution)/shard_map/slice | solution.py:99
  24.8 1.1 %select_reduce_fusion.1 = (bf16[2,64,512]{2,1,0:T(8,128)(2,1)S(1)}, bf16[2,64,512]{2,1,0:T(8,128)(2,1)S(1)}) fusion(bf16[2,2,64,512]{3,2,1,0:T(8,128)(2,1)} %param.19, pred[2]{0:T(512)(128)(4,1)S(1)} %iota_compare_fusion.5, pred[2]{0:T(512)(128)(4,1)S(1)} %iota_compare_fusion.4), kind=kLoop, calls=%fused_computation.70 | loop fusion | flops 393216 | bytes 524292 | tf_op jit(solution)/shard_map/reduce_sum | solution.py:100
  26.0 0.8 %scatter_custom_fusion.1 = s32[64]{0:T(128)S(1)} fusion(s32[64]{0:T(128)S(1)} %get-tuple-element.230, s32[64]{0:T(128)S(1)} %iota.37, s32[]{:T(128)} %constant.130.clone.1), kind=kCustom, calls=%fused_computation.161 | custom fusion | bytes 260 | tf_op jit(solution)/shard_map/scatter | solution.py:51
  26.9 0.6 %compare_and_fusion.2 = (pred[64]{0:T(512)(128)(4,1)S(1)}, s32[64]{0:T(128)S(1)}) fusion(pred[64]{0:T(512)(128)(4,1)S(1)} %lt.139, s32[64]{0:T(128)S(1)} %get-tuple-element.171, s32[]{:T(128)} %convert_reduce_fusion.3, s32[64]{0:T(128)S(1)} %get-tuple-element.169), kind=kLoop, calls=%fused_computation.149 | loop fusion | flops 768 | bytes 900 | tf_op jit(solution)/shard_map/jit(_take)/and | solution.py:70
  27.9 0.7 %compare_and_fusion = (pred[64]{0:T(512)(128)(4,1)S(1)}, s32[64]{0:T(128)S(1)}) fusion(pred[64]{0:T(512)(128)(4,1)S(1)} %lt.145, s32[64]{0:T(128)S(1)} %get-tuple-element.229, s32[]{:T(128)} %convert_reduce_fusion.2, s32[64]{0:T(128)S(1)} %get-tuple-element.231), kind=kLoop, calls=%fused_computation.147 | loop fusion | flops 768 | bytes 900 | tf_op jit(solution)/shard_map/jit(_take)/and | solution.py:70
  30.4 0.6 %gather_fusion = bf16[64,128]{1,0:T(8,128)(2,1)S(1)} fusion(bf16[64,128]{1,0:T(8,128)(2,1)S(1)} %bitcast.118, s32[1024]{0:T(1024)S(1)} %pad_clamp_fusion.3), kind=kCustom, calls=%fused_computation.clone | custom fusion | bytes 33024 | tf_op jit(solution)/shard_map/jit(_take)/gather | solution.py:58
  31.2 7.7 %while.47 = (s32[]{:T(128)}, bf16[64,512]{1,0:T(8,128)(2,1)S(1)}, s32[]{:T(128)}, bf16[64,128]{1,0:T(8,128)(2,1)S(1)}, bf16[128,1024]{1,0:T(8,128)(2,1)S(1)}, /*...) while((s32[]{:T(128)}, bf16[64,512]{1,0:T(8,128)(2,1)S(1)}, ...), condition=%wide.region_9.11_spmd, body=%wide.region_6.10_spmd.sunk | while | flops 17199112 | bytes 1253674 | solution.py:69
  31.2 3.8 %while.50 = (s32[]{:T(128)}, f32[32,1024]{1,0:T(8,128)S(1)}, bf16[128,1024]{1,0:T(8,128)(2,1)S(1)}, f32[32,128]{1,0:T(8,128)S(1)}, s32[]{:T(128)}, /*index=5*/s32[]{:T(128)}) while((s32[]{:T(128)}, f32[32,1024]{1,0:T(8,128)S(1)}, bf16[128,1024]{1,0:T(8,128)(2,1)S(1)}, f32[32,128]{1,0:T(8,128)S(1)}, s32[]{:T(128)}, ...), condition=%wide.region_8.9_spmd.clone, body=%wide.region_7.8_spmd.clone.sunk | while | flops 17129476 | bytes 1065039 | solution.py:40
  31.2 0.4 fusion.128
  31.7 0.4 fusion.128
  32.2 0.4 fusion.128
  32.6 0.4 fusion.128
  33.1 0.4 fusion.128
  33.6 0.4 fusion.128
  34.1 0.4 fusion.128
  34.5 0.4 fusion.128
  35.1 3.8 %while.50 = (s32[]{:T(128)}, f32[32,1024]{1,0:T(8,128)S(1)}, bf16[128,1024]{1,0:T(8,128)(2,1)S(1)}, f32[32,128]{1,0:T(8,128)S(1)}, s32[]{:T(128)}, /*index=5*/s32[]{:T(128)}) while((s32[]{:T(128)}, f32[32,1024]{1,0:T(8,128)S(1)}, bf16[128,1024]{1,0:T(8,128)(2,1)S(1)}, f32[32,128]{1,0:T(8,128)S(1)}, s32[]{:T(128)}, ...), condition=%wide.region_8.9_spmd.clone, body=%wide.region_7.8_spmd.clone.sunk | while | flops 17129476 | bytes 1065039 | solution.py:40
  35.1 0.4 fusion.128
  35.5 0.4 fusion.128
  36.0 0.4 fusion.128
  36.5 0.4 fusion.128
  37.0 0.4 fusion.128
  37.4 0.4 fusion.128
  37.9 0.4 fusion.128
  38.4 0.4 fusion.128
  38.9 0.6 %gather_fusion.2 = bf16[64,128]{1,0:T(8,128)(2,1)S(1)} fusion(bf16[64,128]{1,0:T(8,128)(2,1)S(1)} %bitcast.117, s32[1024]{0:T(1024)S(1)} %pad_clamp_fusion.1), kind=kCustom, calls=%fused_computation.2.clone | custom fusion | bytes 33024 | tf_op jit(solution)/shard_map/jit(_take)/gather | solution.py:58
  39.6 7.7 %while.49 = (s32[]{:T(128)}, bf16[64,512]{1,0:T(8,128)(2,1)S(1)}, s32[]{:T(128)}, bf16[64,128]{1,0:T(8,128)(2,1)S(1)}, bf16[128,1024]{1,0:T(8,128)(2,1)S(1)}, /*...) while((s32[]{:T(128)}, bf16[64,512]{1,0:T(8,128)(2,1)S(1)}, ...), condition=%wide.region_20.23_spmd, body=%wide.region_17.22_spmd.sunk | while | flops 17199112 | bytes 1253674 | solution.py:69
  39.7 3.8 %while.51 = (s32[]{:T(128)}, f32[32,1024]{1,0:T(8,128)S(1)}, bf16[128,1024]{1,0:T(8,128)(2,1)S(1)}, f32[32,128]{1,0:T(8,128)S(1)}, s32[]{:T(128)}, /*index=5*/s32[]{:T(128)}) while((s32[]{:T(128)}, f32[32,1024]{1,0:T(8,128)S(1)}, bf16[128,1024]{1,0:T(8,128)(2,1)S(1)}, f32[32,128]{1,0:T(8,128)S(1)}, s32[]{:T(128)}, ...), condition=%wide.region_19.21_spmd.clone, body=%wide.region_18.20_spmd.clone.sunk | while | flops 17129476 | bytes 1065039 | solution.py:40
  39.7 0.4 fusion.124
  40.1 0.4 fusion.124
  40.6 0.4 fusion.124
  41.1 0.4 fusion.124
  41.6 0.4 fusion.124
  42.0 0.4 fusion.124
  42.5 0.4 fusion.124
  43.0 0.4 fusion.124
  43.5 3.8 %while.51 = (s32[]{:T(128)}, f32[32,1024]{1,0:T(8,128)S(1)}, bf16[128,1024]{1,0:T(8,128)(2,1)S(1)}, f32[32,128]{1,0:T(8,128)S(1)}, s32[]{:T(128)}, /*index=5*/s32[]{:T(128)}) while((s32[]{:T(128)}, f32[32,1024]{1,0:T(8,128)S(1)}, bf16[128,1024]{1,0:T(8,128)(2,1)S(1)}, f32[32,128]{1,0:T(8,128)S(1)}, s32[]{:T(128)}, ...), condition=%wide.region_19.21_spmd.clone, body=%wide.region_18.20_spmd.clone.sunk | while | flops 17129476 | bytes 1065039 | solution.py:40
  43.5 0.4 fusion.124
  44.0 0.4 fusion.124
  44.5 0.4 fusion.124
  44.9 0.4 fusion.124
  45.4 0.4 fusion.124
  45.9 0.4 fusion.124
  46.4 0.4 fusion.124
  46.8 0.4 fusion.124
  47.3 0.7 %gather_fusion.1 = bf16[64,512]{1,0:T(8,128)(2,1)S(1)} fusion(bf16[64,512]{1,0:T(8,128)(2,1)S(1)} %get-tuple-element.133, s32[1024]{0:T(1024)S(1)} %pad_clamp_fusion.2), kind=kCustom, calls=%fused_computation.1.clone | custom fusion | bytes 131328 | tf_op jit(solution)/shard_map/jit(_take)/gather | solution.py:70
  48.1 0.7 %gather_fusion.3 = bf16[64,512]{1,0:T(8,128)(2,1)S(1)} fusion(bf16[64,512]{1,0:T(8,128)(2,1)S(1)} %get-tuple-element.134, s32[1024]{0:T(1024)S(1)} %pad_clamp_fusion), kind=kCustom, calls=%fused_computation.3.clone | custom fusion | bytes 131328 | tf_op jit(solution)/shard_map/jit(_take)/gather | solution.py:70
  48.9 0.7 %convolution_bitcast_fusion.1 = f32[2,1024,256]{2,1,0:T(8,128)S(1)} fusion(bf16[128,2,2,256]{3,0,1,2:T(8,128)(2,1)S(1)} %bitcast.115, bf16[64,64]{1,0:T(8,128)(2,1)S(1)} %get-tuple-element.236, bf16[64,64]{1,0:T(8,128)(2,1)S(1)} %get-tuple-element.237, bf16[64,64]{1,0:T(8,128)(2,1)S(1)} %get-tuple-element.238, bf16[64,512]{1,0:T(8,128)(2,1)S(1)} %get-tuple-element.232, ...), kind=kOutput, calls=%fused_computation.47 | convolution fusion | flops 152240128 | bytes 2473984 | tf_op jit(solution)/shard_map/ie,iap->aep/dot_general | solution.py:115
  50.0 0.7 %convolution_bitcast_fusion = f32[2,1024,256]{2,1,0:T(8,128)S(1)} fusion(bf16[128,2,2,256]{3,0,1,2:T(8,128)(2,1)S(1)} %bitcast.116, bf16[64,64]{1,0:T(8,128)(2,1)S(1)} %get-tuple-element.224, bf16[64,64]{1,0:T(8,128)(2,1)S(1)} %get-tuple-element.223, bf16[64,64]{1,0:T(8,128)(2,1)S(1)} %get-tuple-element.239, bf16[64,512]{1,0:T(8,128)(2,1)S(1)} %get-tuple-element.220, ...), kind=kOutput, calls=%fused_computation.46 | convolution fusion | flops 152240128 | bytes 2473984 | tf_op jit(solution)/shard_map/ie,iap->aep/dot_general | solution.py:115
  51.1 1.0 %copy.22 = bf16[2,2,512,256]{3,2,1,0:T(8,128)(2,1)} copy(bf16[2,2,512,256]{3,2,0,1:T(8,128)(2,1)S(1)} %pad_maximum_fusion) | data formatting | bytes 2097152 | tf_op jit(solution)/shard_map/stack | solution.py:145
  (131 shorter events, 4.5 us)
Async XLA Ops:
  0.0 26.9 %copy-start.1 = (s32[2,2,32]{2,1,0:T(2,128)S(1)}, s32[2,2,32]{2,1,0:T(2,128)}, u32[]{:S(2)}) copy-start(s32[2,2,32]{2,1,0:T(2,128)} %param.22) | copy-start | bytes 1540
  0.0 27.5 %copy-start = (bf16[2,2,64,64]{3,2,1,0:T(8,128)(2,1)S(1)}, bf16[2,2,64,64]{3,2,1,0:T(8,128)(2,1)}, u32[]{:S(2)}) copy-start(bf16[2,2,64,64]{3,2,1,0:T(8,128)(2,1)} %param.20) | copy-start | bytes 98308
  11.2 18.8 %all-to-all-start = ((bf16[8,2,1,8,2,2,256]{6,5,4,3,1,2,0:T(2,128)(2,1)}), bf16[8,2,1,8,2,2,256]{6,5,4,3,1,2,0:T(2,128)(2,1)S(1)}, u32[]{:S(2)}, u32[]{:S(2)}) async-start(bf16[8,2,1,8,2,2,256]{6,5,4,3,1,2,0:T(2,128)(2,1)} %fusion.48), calls=%async_computation | async-start | bytes 524288 | tf_op jit(solution)/shard_map/all_to_all | solution.py:76
